TPU v7x, 512 devices: a whole 4x8x8 slice. The times are simulated.
512 devices in a mesh: section: 16 (over x_hi, z), mp: 32 (over y, x_lo, core).
Axes of the slice: x: 4 (x_hi: 2, x_lo: 2; x = x_hi * 2 + x_lo), y: 8, z: 8, core: 2. Of those that a mesh axis runs over, the one named last changes fastest.
Arguments:
- embeddings: bfloat16 [16, 4, 128, 4096], P('section', None, None, 'mp'), may hold values from -6 to 6
- stored: bfloat16 [16, 15, 128, 4096], P('section', None, None, 'mp'), may hold values from -6 to 6
- dwa_weights: float32 [16, 16], replicated, may hold values from -2.4 to 2.4
- norm_gain: float32 [16, 4096], P('section'), may hold values from 0.5 to 1.5
- qkv_weight: bfloat16 [16, 4096, 3, 4096], P('section', None, None, 'mp')
- out_weight: bfloat16 [16, 4096, 4096], P('section', None, 'mp'), may hold values from -0.09375 to 0.09375
Outputs:
- layer_outputs: bfloat16 [16, 4, 128, 4096], P('section', None, None, 'mp')
All inputs are finite; a program needn't handle non-finite values.
Results may differ from a plain program's by a relative error of at most 0.014.
Values may be sent and summed in bfloat16 or wider, within the bound.
No kernel may reach another device: no remote copies, remote signals or barrier semaphores. Data moves between devices by JAX's collectives and lax.ppermute only.
A program may use at most 64 MiB of HBM per device.

v0:
```python
import jax
import jax.numpy as jnp
from jax import lax
from jax.sharding import PartitionSpec as P

D = 4096
HEAD_DIM = 128


EPS = 1e-06


def copy_for_each(x, axis):
    devices = lax.axis_size(axis)
    return lax.all_to_all(jnp.broadcast_to(x[None], (devices, *x.shape)), axis, 0, 0, tiled=True)


def joined_along(pieces, dim):
    pieces = jnp.moveaxis(pieces, 0, dim)
    dims = pieces.shape
    return pieces.reshape(*dims[:dim], dims[dim] * dims[dim + 1], *dims[dim + 2 :])


def gather_directly(x, axis, dim):
    pieces = copy_for_each(x, axis)
    return joined_along(pieces, dim)


def attend_heads(projected):
    length = projected.shape[0]
    query = projected[:, 0].astype(jnp.float32)
    key_rows = projected[:, 1].astype(jnp.float32)
    value_rows = projected[:, 2].astype(jnp.float32)
    scores = jnp.einsum("qhd,khd->hqk", query, key_rows) * projected.shape[3] ** (-0.5)
    causal = lax.broadcasted_iota(jnp.int32, (length, length), 0) >= lax.broadcasted_iota(
        jnp.int32, (length, length), 1
    )
    scores = jnp.where(causal[None], scores, -1e30)
    row_max = jnp.max(scores, axis=2, keepdims=True)
    weights = jnp.exp(scores - row_max)
    probs = (weights / jnp.sum(weights, axis=2, keepdims=True)).astype(jnp.bfloat16)
    mixed = jnp.einsum("hqk,khd->qhd", probs.astype(jnp.float32), value_rows)
    return mixed.astype(jnp.bfloat16).reshape(length, -1)


def local(embeddings, stored, dwa_weights, norm_gain, qkv_weight, out_weight):
    sections = lax.axis_size("section")
    section_rank = lax.axis_index("section")
    tick_count = embeddings.shape[1]
    length = embeddings.shape[2]
    shard_width = embeddings.shape[3]
    heads_here = shard_width // HEAD_DIM
    triangle = jnp.tril(jnp.ones((sections, sections), jnp.float32))
    mixing = dwa_weights * triangle
    own_row = lax.dynamic_index_in_dim(mixing, section_rank, 0, keepdims=False)
    history = jnp.concatenate(
        [stored[0], jnp.zeros((tick_count, length, shard_width), jnp.bfloat16)], axis=0
    )
    gain_row = norm_gain[0]
    weight_in = qkv_weight[0].reshape(D, 3 * shard_width)
    weight_out = out_weight[0]
    results = []
    for step_index in range(tick_count):
        own_embed = own_row[0] * embeddings[0, step_index].astype(jnp.float32)
        outgoing = lax.slice_in_dim(history, step_index, step_index + sections, axis=0)[::-1]
        incoming = lax.all_to_all(outgoing, "section", split_axis=0, concat_axis=0, tiled=True)
        summed = own_embed + jnp.tensordot(own_row[1:], incoming[:-1].astype(jnp.float32), axes=1)
        inputs = summed.astype(jnp.bfloat16)
        gathered = gather_directly(inputs, "mp", 1)
        values = gathered.astype(jnp.float32)
        inverse = lax.rsqrt(jnp.mean(values * values, axis=1, keepdims=True) + EPS)
        normed = (values * inverse * gain_row).astype(jnp.bfloat16)
        projected = jnp.dot(normed, weight_in, preferred_element_type=jnp.float32).astype(
            jnp.bfloat16
        )
        projected = projected.reshape(length, 3, heads_here, HEAD_DIM)
        mixed = attend_heads(projected)
        attn = jnp.dot(
            gather_directly(mixed, "mp", 1), weight_out, preferred_element_type=jnp.float32
        )
        fresh_rows = (inputs.astype(jnp.float32) + attn).astype(jnp.bfloat16)
        slot_index = step_index + sections - 1 - section_rank
        history = lax.dynamic_update_slice_in_dim(history, fresh_rows[None], slot_index, 0)
        results.append(fresh_rows)
    return jnp.stack(results)[None]


def solution(mesh):
    in_specs = (
        P("section", None, None, "mp"),
        P("section", None, None, "mp"),
        P(),
        P("section", None),
        P("section", None, None, "mp"),
        P("section", None, "mp"),
    )
    out_specs = P("section", None, None, "mp")
    return jax.shard_map(local, mesh=mesh, in_specs=in_specs, out_specs=out_specs, check_vma=False)
```

profile of v0, /device:TPU:1, one launch (start us, length us, event | category | flops | bytes accessed | tf_op | source)
XLA Modules:
  0.0 385.8 jit_solution(17109009062536009105)
XLA Ops:
  0.0 1.2 pad_slice_fusion
  2.0 13.4 %all-to-all-start = ((bf16[16,128,128]{2,1,0:T(8,128)(2,1)}), bf16[16,128,128]{2,1,0:T(8,128)(2,1)S(1)}, u32[]{:S(2)}, u32[]{:S(2)}) async-start(bf16[16,128,128]{2,1,0:T(8,128)(2,1)} %rev.12), calls=%async_computation | async-start | bytes 1048576 | tf_op jit(solution)/shard_map/all_to_all | solution.py:66
  16.1 14.6 %all-to-all-done = bf16[16,128,128]{2,1,0:T(8,128)(2,1)S(1)} async-done(((bf16[16,128,128]{2,1,0:T(8,128)(2,1)}), bf16[16,128,128]{2,1,0:T(8,128)(2,1)S(1)}, u32[]{:S(2)}, u32[]{:S(2)}) %all-to-all-start) | async-done | bytes 524320 | tf_op jit(solution)/shard_map/all_to_all | solution.py:66
  31.3 1.2 broadcast_in_dim.41
  32.6 10.1 %all-to-all-start.1 = ((bf16[32,128,128]{1,2,0:T(8,128)(2,1)}), bf16[32,128,128]{1,2,0:T(8,128)(2,1)S(1)}, u32[]{:S(2)}, u32[]{:S(2)}) async-start(bf16[32,128,128]{1,2,0:T(8,128)(2,1)} %broadcast_in_dim.41), calls=%async_computation.1 | async-start | bytes 2097152 | tf_op jit(solution)/shard_map/all_to_all | solution.py:15
  42.7 4.7 %copy.12 = bf16[1,4096,3,128]{1,3,2,0:T(8,128)(2,1)} copy(bf16[1,4096,3,128]{3,1,2,0:T(8,128)(2,1)} %param.10) | data formatting | bytes 6291456 | tf_op args[4]
  47.4 23.4 %all-to-all-done.1 = bf16[32,128,128]{1,2,0:T(8,128)(2,1)S(1)} async-done(((bf16[32,128,128]{1,2,0:T(8,128)(2,1)}), bf16[32,128,128]{1,2,0:T(8,128)(2,1)S(1)}, u32[]{:S(2)}, u32[]{:S(2)}) %all-to-all-start.1) | async-done | bytes 1048608 | tf_op jit(solution)/shard_map/all_to_all | solution.py:15
  74.3 1.2 broadcast_in_dim.44
  75.5 4.3 %all-to-all-start.2 = ((bf16[32,128,128]{1,2,0:T(8,128)(2,1)}), bf16[32,128,128]{1,2,0:T(8,128)(2,1)S(1)}, u32[]{:S(2)}, u32[]{:S(2)}) async-start(bf16[32,128,128]{1,2,0:T(8,128)(2,1)} %broadcast_in_dim.44), calls=%async_computation.2 | async-start | bytes 2097152 | tf_op jit(solution)/shard_map/all_to_all | solution.py:15
  79.9 27.9 %all-to-all-done.2 = bf16[32,128,128]{1,2,0:T(8,128)(2,1)S(1)} async-done(((bf16[32,128,128]{1,2,0:T(8,128)(2,1)}), bf16[32,128,128]{1,2,0:T(8,128)(2,1)S(1)}, u32[]{:S(2)}, u32[]{:S(2)}) %all-to-all-start.2) | async-done | bytes 1048608 | tf_op jit(solution)/shard_map/all_to_all | solution.py:15
  108.5 19.2 %all_to_all.60 = bf16[16,128,128]{2,1,0:T(8,128)(2,1)S(1)} all-to-all(bf16[16,128,128]{2,1,0:T(8,128)(2,1)S(1)} %rev.13), channel_id=1, replica_groups=mesh['section'=16,'mp'=32] {'section'}, dimensions={0} | all-to-all | bytes 1048576 | tf_op jit(solution)/shard_map/all_to_all | solution.py:66
  128.6 35.0 %all_to_all.61 = bf16[32,128,128]{1,2,0:T(8,128)(2,1)S(1)} all-to-all(bf16[32,128,128]{1,2,0:T(8,128)(2,1)S(1)} %broadcast_in_dim.45), channel_id=1, replica_groups=mesh['section'=16,'mp'=32] {'mp'}, dimensions={0} | all-to-all | bytes 2097152 | tf_op jit(solution)/shard_map/all_to_all | solution.py:15
  167.0 1.2 broadcast_in_dim.47
  168.3 4.3 %all-to-all-start.5 = ((bf16[32,128,128]{1,2,0:T(8,128)(2,1)}), bf16[32,128,128]{1,2,0:T(8,128)(2,1)S(1)}, u32[]{:S(2)}, u32[]{:S(2)}) async-start(bf16[32,128,128]{1,2,0:T(8,128)(2,1)} %broadcast_in_dim.47), calls=%async_computation.5 | async-start | bytes 2097152 | tf_op jit(solution)/shard_map/all_to_all | solution.py:15
  172.6 28.0 %all-to-all-done.5 = bf16[32,128,128]{1,2,0:T(8,128)(2,1)S(1)} async-done(((bf16[32,128,128]{1,2,0:T(8,128)(2,1)}), bf16[32,128,128]{1,2,0:T(8,128)(2,1)S(1)}, u32[]{:S(2)}, u32[]{:S(2)}) %all-to-all-start.5) | async-done | bytes 1048608 | tf_op jit(solution)/shard_map/all_to_all | solution.py:15
  201.2 19.1 %all_to_all.62 = bf16[16,128,128]{2,1,0:T(8,128)(2,1)S(1)} all-to-all(bf16[16,128,128]{2,1,0:T(8,128)(2,1)S(1)} %rev.14), channel_id=1, replica_groups=mesh['section'=16,'mp'=32] {'section'}, dimensions={0} | all-to-all | bytes 1048576 | tf_op jit(solution)/shard_map/all_to_all | solution.py:66
  221.2 34.8 %all_to_all.63 = bf16[32,128,128]{1,2,0:T(8,128)(2,1)S(1)} all-to-all(bf16[32,128,128]{1,2,0:T(8,128)(2,1)S(1)} %broadcast_in_dim.48), channel_id=1, replica_groups=mesh['section'=16,'mp'=32] {'mp'}, dimensions={0} | all-to-all | bytes 2097152 | tf_op jit(solution)/shard_map/all_to_all | solution.py:15
  259.4 1.2 broadcast_in_dim.50
  260.7 4.5 %all-to-all-start.8 = ((bf16[32,128,128]{1,2,0:T(8,128)(2,1)}), bf16[32,128,128]{1,2,0:T(8,128)(2,1)S(1)}, u32[]{:S(2)}, u32[]{:S(2)}) async-start(bf16[32,128,128]{1,2,0:T(8,128)(2,1)} %broadcast_in_dim.50), calls=%async_computation.8 | async-start | bytes 2097152 | tf_op jit(solution)/shard_map/all_to_all | solution.py:15
  265.2 28.0 %all-to-all-done.8 = bf16[32,128,128]{1,2,0:T(8,128)(2,1)S(1)} async-done(((bf16[32,128,128]{1,2,0:T(8,128)(2,1)}), bf16[32,128,128]{1,2,0:T(8,128)(2,1)S(1)}, u32[]{:S(2)}, u32[]{:S(2)}) %all-to-all-start.8) | async-done | bytes 1048608 | tf_op jit(solution)/shard_map/all_to_all | solution.py:15
  293.9 19.6 %all_to_all.64 = bf16[16,128,128]{2,1,0:T(8,128)(2,1)S(1)} all-to-all(bf16[16,128,128]{2,1,0:T(8,128)(2,1)S(1)} %rev.15), channel_id=1, replica_groups=mesh['section'=16,'mp'=32] {'section'}, dimensions={0} | all-to-all | bytes 1048576 | tf_op jit(solution)/shard_map/all_to_all | solution.py:66
  314.3 34.4 %all_to_all.65 = bf16[32,128,128]{1,2,0:T(8,128)(2,1)S(1)} all-to-all(bf16[32,128,128]{1,2,0:T(8,128)(2,1)S(1)} %broadcast_in_dim.51), channel_id=1, replica_groups=mesh['section'=16,'mp'=32] {'mp'}, dimensions={0} | all-to-all | bytes 2097152 | tf_op jit(solution)/shard_map/all_to_all | solution.py:15
  350.6 1.1 convolution_convert_fusion
  352.4 32.2 %all_to_all.66 = bf16[32,128,128]{1,2,0:T(8,128)(2,1)S(1)} all-to-all(bf16[32,128,128]{1,2,0:T(8,128)(2,1)S(1)} %broadcast_in_dim.53), channel_id=1, replica_groups=mesh['section'=16,'mp'=32] {'mp'}, dimensions={0} | all-to-all | bytes 2097152 | tf_op jit(solution)/shard_map/all_to_all | solution.py:15
  (81 shorter events, 20.6 us)
Async XLA Ops:
  0.0 107.9 %copy-start = (bf16[1,4096,128]{2,1,0:T(8,128)(2,1)S(1)}, bf16[1,4096,128]{2,1,0:T(8,128)(2,1)}, u32[]{:S(2)}) copy-start(bf16[1,4096,128]{2,1,0:T(8,128)(2,1)} %param.11) | copy-start | bytes 3145732
  1.2 30.0 %copy-start.7 = (bf16[1,4,128,128]{3,2,1,0:T(8,128)(2,1)S(1)}, bf16[1,4,128,128]{3,2,1,0:T(8,128)(2,1)}, u32[]{:S(2)}) copy-start(bf16[1,4,128,128]{3,2,1,0:T(8,128)(2,1)} %param.6) | copy-start | bytes 393220
  2.0 28.7 %all-to-all-start = ((bf16[16,128,128]{2,1,0:T(8,128)(2,1)}), bf16[16,128,128]{2,1,0:T(8,128)(2,1)S(1)}, u32[]{:S(2)}, u32[]{:S(2)}) async-start(bf16[16,128,128]{2,1,0:T(8,128)(2,1)} %rev.12), calls=%async_computation | async-start | bytes 1048576 | tf_op jit(solution)/shard_map/all_to_all | solution.py:66
  32.6 38.2 %all-to-all-start.1 = ((bf16[32,128,128]{1,2,0:T(8,128)(2,1)}), bf16[32,128,128]{1,2,0:T(8,128)(2,1)S(1)}, u32[]{:S(2)}, u32[]{:S(2)}) async-start(bf16[32,128,128]{1,2,0:T(8,128)(2,1)} %broadcast_in_dim.41), calls=%async_computation.1 | async-start | bytes 2097152 | tf_op jit(solution)/shard_map/all_to_all | solution.py:15
  42.7 28.6 %copy-start.6 = (f32[1,4096]{1,0:T(1,128)S(1)}, f32[1,4096]{1,0:T(1,128)}, u32[]{:S(2)}) copy-start(f32[1,4096]{1,0:T(1,128)} %param.9) | copy-start | bytes 49156
  70.8 1.9 copy-start.1
  73.7 6.1 %copy-start.5 = (bf16[1,15,128,128]{3,2,1,0:T(8,128)(2,1)S(1)}, bf16[1,15,128,128]{3,2,1,0:T(8,128)(2,1)}, u32[]{:S(2)}) copy-start(bf16[1,15,128,128]{3,2,1,0:T(8,128)(2,1)} %param.7) | copy-start | bytes 1474564
  75.5 32.3 %all-to-all-start.2 = ((bf16[32,128,128]{1,2,0:T(8,128)(2,1)}), bf16[32,128,128]{1,2,0:T(8,128)(2,1)S(1)}, u32[]{:S(2)}, u32[]{:S(2)}) async-start(bf16[32,128,128]{1,2,0:T(8,128)(2,1)} %broadcast_in_dim.44), calls=%async_computation.2 | async-start | bytes 2097152 | tf_op jit(solution)/shard_map/all_to_all | solution.py:15
  163.5 1.9 copy-start.2
  168.3 32.3 %all-to-all-start.5 = ((bf16[32,128,128]{1,2,0:T(8,128)(2,1)}), bf16[32,128,128]{1,2,0:T(8,128)(2,1)S(1)}, u32[]{:S(2)}, u32[]{:S(2)}) async-start(bf16[32,128,128]{1,2,0:T(8,128)(2,1)} %broadcast_in_dim.47), calls=%async_computation.5 | async-start | bytes 2097152 | tf_op jit(solution)/shard_map/all_to_all | solution.py:15
  255.9 1.9 copy-start.3
  260.7 32.6 %all-to-all-start.8 = ((bf16[32,128,128]{1,2,0:T(8,128)(2,1)}), bf16[32,128,128]{1,2,0:T(8,128)(2,1)S(1)}, u32[]{:S(2)}, u32[]{:S(2)}) async-start(bf16[32,128,128]{1,2,0:T(8,128)(2,1)} %broadcast_in_dim.50), calls=%async_computation.8 | async-start | bytes 2097152 | tf_op jit(solution)/shard_map/all_to_all | solution.py:15
  348.7 1.9 copy-start.4
where the time goes:
time: 387 us; the launch traced here: 386 us
  blocking collectives  194 us (50%)
  waiting for transfers between devices  122 us (32%)
  starting transfers between devices  36.7 us (9%)
  local copies, waits for them, and re-layouts  16.4 us (4%)
  matrix products  9.23 us (2%)
  other arithmetic  6.82 us (2%)
    all_to_all x4, blocking collectives, copy_for_each(): lax.all_to_all(jnp.broadcast_to(x[None], (devices, *x.shape)), axis, 0, 0...  136 us
    all_to_all x4, waiting for transfers between devices, copy_for_each(): lax.all_to_all(jnp.broadcast_to(x[None], (devices, *x.shape)), axis, 0, 0...  107 us
    all_to_all x3, blocking collectives, local(): lax.all_to_all(outgoing, 'section', split_axis=0, concat_axis=0, tiled=True)  57.9 us
    all_to_all x4, starting transfers between devices, copy_for_each(): lax.all_to_all(jnp.broadcast_to(x[None], (devices, *x.shape)), axis, 0, 0...  23.3 us
    all_to_all x1, waiting for transfers between devices, local(): lax.all_to_all(outgoing, 'section', split_axis=0, concat_axis=0, tiled=True)  14.6 us
    all_to_all x1, starting transfers between devices, local(): lax.all_to_all(outgoing, 'section', split_axis=0, concat_axis=0, tiled=True)  13.4 us
  transfers between devices with their start and end apart: 5, of which 5 were waited for; matrix products, arithmetic and copies ran while one was open for 1% of the time, Pallas kernels for 0%

commit v1 on v0

v1 whole, which is shorter than its diff:
```python
import jax
import jax.numpy as jnp
from jax import lax
from jax.sharding import Mesh, PartitionSpec as P

HEAD_DIM = 128
EPS = 1e-06
CORE_SWAP = ((0, 1), (1, 0))

SECTION = ("xh", "z")
CHIPS = ("y", "xl")


def spread(piece, axis):
    count = lax.axis_size(axis)
    return lax.all_to_all(jnp.broadcast_to(piece[None], (count, *piece.shape)), axis, 0, 0, tiled=True)


def in_core_order(core, own, other):
    return jnp.where(core == 0, jnp.stack([own, other]), jnp.stack([other, own]))


def attend(core, projected, partner_projected):
    tokens = projected.shape[0]
    pair = jnp.stack([projected, partner_projected])
    pair = pair.reshape(2, tokens, 3, HEAD_DIM)
    both = lax.all_gather(pair[:, :, 1:], "c")
    other = lax.dynamic_index_in_dim(both, 1 - core, 0, keepdims=False)[::-1]
    query = pair[:, :, 0]
    scale = HEAD_DIM ** (-0.5)
    dims = (((2,), (2,)), ((0,), (0,)))
    near = lax.dot_general(query, pair[:, :, 1], dims, preferred_element_type=jnp.float32) * scale
    far = lax.dot_general(query, other[:, :, 0], dims, preferred_element_type=jnp.float32) * scale
    row = lax.broadcasted_iota(jnp.int32, (tokens, tokens), 0)
    col = lax.broadcasted_iota(jnp.int32, (tokens, tokens), 1)
    near = jnp.where((row >= col)[None], near, -1e30)
    far = jnp.where(core == 1, far, -1e30)
    top = jnp.maximum(jnp.max(near, axis=2, keepdims=True), jnp.max(far, axis=2, keepdims=True))
    near = jnp.exp(near - top)
    far = jnp.exp(far - top)
    total = jnp.sum(near, axis=2, keepdims=True) + jnp.sum(far, axis=2, keepdims=True)
    near = (near / total).astype(jnp.bfloat16)
    far = (far / total).astype(jnp.bfloat16)
    dims = (((2,), (1,)), ((0,), (0,)))
    mixed = lax.dot_general(near, pair[:, :, 2], dims, preferred_element_type=jnp.float32)
    mixed = mixed + lax.dot_general(far, other[:, :, 1], dims, preferred_element_type=jnp.float32)
    mixed = mixed.astype(jnp.bfloat16)
    return in_core_order(core, mixed[0], mixed[1])


def local(embeddings, stored, dwa_weights, norm_gain, qkv_weight, out_weight):
    sections = lax.axis_size(SECTION)
    rank = lax.axis_index(SECTION)
    core = lax.axis_index("c")
    ticks, length, width = embeddings.shape[1:]
    half = length // 2
    features = norm_gain.shape[1]
    blocks = features // width
    forward = tuple((s, s + 1) for s in range(sections - 1))

    mixing = dwa_weights * jnp.tril(jnp.ones((sections, sections), jnp.float32))
    mixing = jnp.concatenate([mixing, jnp.zeros((ticks, sections), jnp.float32)], axis=0)
    rows = lax.dynamic_slice_in_dim(mixing, rank, ticks, axis=0)
    newest = lax.dynamic_index_in_dim(rows, rank, 1, keepdims=False)

    weight_in = qkv_weight[0].reshape(features, 3 * width)
    weight_out = out_weight[0]
    partner_in = lax.ppermute(weight_in, "c", CORE_SWAP)
    partner_out = lax.ppermute(weight_out, "c", CORE_SWAP)
    gain = norm_gain[0].reshape(blocks, 1, width)

    target = lax.broadcasted_iota(jnp.int32, (sections, 1, 1), 0)
    outgoing = jnp.concatenate([stored[0], embeddings[0, :1]], axis=0)[::-1]
    outgoing = jnp.where(target == rank, embeddings[0, :1], outgoing)
    incoming = lax.all_to_all(
        outgoing.reshape(sections * 2, half, width), SECTION + ("c",), 0, 0, tiled=True
    )
    incoming = incoming.reshape(sections, 2, half, width).astype(jnp.float32)
    source = lax.broadcasted_iota(jnp.int32, (1, sections), 1)
    shifted = jnp.concatenate([rows[:, 1:], jnp.zeros((ticks, 1), jnp.float32)], axis=1)
    weights = jnp.where(source < rank, shifted, 0.0)
    first = jnp.where(source[0] == rank, rows[0, 0], weights[0])
    summed = jnp.sum(first[:, None, None, None] * incoming, axis=0)
    later = [
        jnp.sum(weights[r][:, None, None, None] * incoming, axis=0) for r in range(1, ticks)
    ]

    embedded = lax.all_gather(embeddings[0, 1:].reshape(ticks - 1, 2, half, width), "c")
    embedded = lax.dynamic_index_in_dim(embedded, core, 2, keepdims=False)

    results = []
    for tick in range(ticks):
        if tick:
            summed = rows[0, 0] * embedded[:, tick - 1].astype(jnp.float32)
            summed = summed + carried[0] + newest[0] * fresh.astype(jnp.float32)
            later = [
                carried[r] + newest[r] * fresh.astype(jnp.float32) for r in range(1, ticks - tick)
            ]
        inputs = summed.astype(jnp.bfloat16)
        if later:
            carried = lax.ppermute(jnp.stack(later), SECTION, forward)
        values = spread(inputs, CHIPS).reshape(blocks, half, width).astype(jnp.float32)
        inverse = lax.rsqrt(jnp.mean(values * values, axis=(0, 2), keepdims=True) + EPS)
        normed = (values * inverse * gain).astype(jnp.bfloat16)
        normed = jnp.transpose(normed, (1, 0, 2)).reshape(half, features)
        projected = jnp.dot(normed, weight_in, preferred_element_type=jnp.float32)
        partner_projected = jnp.dot(normed, partner_in, preferred_element_type=jnp.float32)
        mixed = attend(core, projected.astype(jnp.bfloat16), partner_projected.astype(jnp.bfloat16))
        mixed = spread(mixed, CHIPS).reshape(blocks, half, width)
        mixed = jnp.transpose(mixed, (1, 0, 2)).reshape(half, features)
        attn = jnp.dot(mixed, weight_out, preferred_element_type=jnp.float32)
        partner_attn = jnp.dot(mixed, partner_out, preferred_element_type=jnp.float32)
        attn = in_core_order(core, attn, partner_attn)
        made = (inputs.astype(jnp.float32) + attn).astype(jnp.bfloat16)
        results.append(made)
        if tick + 1 < ticks:
            fresh = lax.ppermute(made, SECTION, forward)
    both = lax.all_gather(jnp.stack(results), "c")
    mine = lax.dynamic_index_in_dim(both, core, 2, keepdims=False)
    return jnp.transpose(mine, (1, 0, 2, 3)).reshape(1, ticks, length, width)


def solution(mesh):
    split = Mesh(mesh.devices.reshape(2, 8, 8, 2, 2), ("xh", "z", "y", "xl", "c"))
    mp = ("y", "xl", "c")
    in_specs = (
        P(SECTION, None, None, mp),
        P(SECTION, None, None, mp),
        P(),
        P(SECTION, None),
        P(SECTION, None, None, mp),
        P(SECTION, None, mp),
    )
    out_specs = P(SECTION, None, None, mp)
    return jax.shard_map(local, mesh=split, in_specs=in_specs, out_specs=out_specs, check_vma=False)
```

time: 387 us -> 339 us (0.88)
  the two profiles are of different devices: /device:TPU:1 before, /device:TPU:5 now
where the time goes in v1:
time: 339 us; the launch traced here: 336 us
  waiting for transfers between devices  88.5 us (26%)
  blocking collectives  84.8 us (25%)
  starting transfers between devices  55.9 us (16%)
  matrix products  44.3 us (13%)
  local copies, waits for them, and re-layouts  35.6 us (11%)
  other arithmetic  25.7 us (8%)
    all_to_all x5, waiting for transfers between devices, spread(): lax.all_to_all(jnp.broadcast_to(piece[None], (count, *piece.shape)), axis...  62.9 us
    all_to_all x3, blocking collectives, spread(): lax.all_to_all(jnp.broadcast_to(piece[None], (count, *piece.shape)), axis...  55.4 us
    all_to_all x5, starting transfers between devices, spread(): lax.all_to_all(jnp.broadcast_to(piece[None], (count, *piece.shape)), axis...  23.9 us
    all_gather x4, blocking collectives, attend(): both = lax.all_gather(pair[:, :, 1:], 'c')  22.4 us
    ppermute x3, waiting for transfers between devices, local(): fresh = lax.ppermute(made, SECTION, forward)  17.3 us
    dot_general x4, matrix products, local(): jnp.dot(normed, partner_in, preferred_element_type=jnp.float32)  14.5 us
    all_to_all x1, starting transfers between devices, local(): lax.all_to_all(outgoing.reshape(sections * 2, half, width), SECTION + ('c...  13.8 us
    unnamed x35, local copies, waits for them, and re-layouts  9.7 us
  transfers between devices with their start and end apart: 14, of which 9 were waited for; matrix products, arithmetic and copies ran while one was open for 9% of the time, Pallas kernels for 0%

profile of v1, /device:TPU:5, one launch (start us, length us, event | category | flops | bytes accessed | tf_op | source)
XLA Modules:
  0.0 335.7 jit_solution(13312192346439107349)
XLA Ops:
  2.8 13.8 %all-to-all-start = ((bf16[32,64,128]{2,1,0:T(8,128)(2,1)}), bf16[32,64,128]{2,1,0:T(8,128)(2,1)}, u32[]{:S(2)}, u32[]{:S(2)}) async-start(bf16[32,64,128]{2,1,0:T(8,128)(2,1)} %bitcast.5), calls=%async_computation | async-start | bytes 1048576 | tf_op jit(solution)/shard_map/all_to_all | solution.py:75
  24.0 8.3 %all-to-all-done = bf16[32,64,128]{2,1,0:T(8,128)(2,1)} async-done(((bf16[32,64,128]{2,1,0:T(8,128)(2,1)}), bf16[32,64,128]{2,1,0:T(8,128)(2,1)}, u32[]{:S(2)}, u32[]{:S(2)}) %all-to-all-start) | async-done | bytes 524320 | tf_op jit(solution)/shard_map/all_to_all | solution.py:75
  35.7 7.6 %all-to-all-start.1 = ((bf16[16,2,64,128]{3,1,2,0:T(2,128)(2,1)}), bf16[16,2,64,128]{3,1,2,0:T(2,128)(2,1)}, u32[]{:S(2)}, u32[]{:S(2)}) async-start(bf16[16,2,64,128]{3,1,2,0:T(2,128)(2,1)} %broadcast_in_dim.159), calls=%async_computation.1 | async-start | bytes 1048576 | tf_op jit(solution)/shard_map/all_to_all | solution.py:16
  43.9 13.9 %all-to-all-done.1 = bf16[16,2,64,128]{3,1,2,0:T(2,128)(2,1)} async-done(((bf16[16,2,64,128]{3,1,2,0:T(2,128)(2,1)}), bf16[16,2,64,128]{3,1,2,0:T(2,128)(2,1)}, u32[]{:S(2)}, u32[]{:S(2)}) %all-to-all-start.1) | async-done | bytes 524320 | tf_op jit(solution)/shard_map/all_to_all | solution.py:16
  63.1 3.8 %convolution_convert_fusion.6 = bf16[64,384]{1,0:T(8,128)(2,1)} fusion(bf16[4096,384]{0,1:T(8,128)(2,1)} %collective-permute-done, bf16[32,64,128]{2,1,0:T(8,128)(2,1)} %copy-done.1), kind=kOutput, calls=%fused_computation.10 | convolution fusion | flops 201351168 | bytes 3719168 | tf_op jit(solution)/shard_map/dot_general | solution.py:107
  69.1 5.6 %all-gather = bf16[4,64,2,128]{3,1,0,2:T(8,128)(2,1)S(1)} all-gather(bf16[2,64,2,128]{3,1,0,2:T(8,128)(2,1)S(1)} %slice.252), channel_id=2, replica_groups=mesh['xh'=2,'z'=8,'y'=8,'xl'=2,'c'=2] {'c'}, dimensions={0}, use_global_device_ids=true | all-gather | bytes 196608 | tf_op jit(solution)/shard_map/all_gather | solution.py:27
  80.5 4.2 %all-to-all-start.2 = ((bf16[16,2,64,128]{3,1,2,0:T(2,128)(2,1)}), bf16[16,2,64,128]{3,1,2,0:T(2,128)(2,1)}, u32[]{:S(2)}, u32[]{:S(2)}) async-start(bf16[16,2,64,128]{3,1,2,0:T(2,128)(2,1)} %broadcast_in_dim.161), calls=%async_computation.2 | async-start | bytes 1048576 | tf_op jit(solution)/shard_map/all_to_all | solution.py:16
  95.0 6.0 %all-to-all-done.2 = bf16[16,2,64,128]{3,1,2,0:T(2,128)(2,1)} async-done(((bf16[16,2,64,128]{3,1,2,0:T(2,128)(2,1)}), bf16[16,2,64,128]{3,1,2,0:T(2,128)(2,1)}, u32[]{:S(2)}, u32[]{:S(2)}) %all-to-all-start.2) | async-done | bytes 524320 | tf_op jit(solution)/shard_map/all_to_all | solution.py:16
  108.9 4.7 %collective-permute-done.3 = bf16[2,64,128]{2,1,0:T(8,128)(2,1)S(1)} collective-permute-done((bf16[2,64,128]{2,1,0:T(8,128)(2,1)S(1)}, bf16[2,64,128]{2,1,0:T(8,128)(2,1)S(1)}, u32[]{:S(2)}, u32[]{:S(2)}) %collective-permute-start.3) | collective-permute-done | bytes 32800 | tf_op jit(solution)/shard_map/ppermute | solution.py:117
  113.5 4.1 %fusion.68 = (f32[1,2,64,128]{3,2,1,0:T(8,128)}, f32[1,2,64,128]{3,2,1,0:T(8,128)}, bf16[2,64,128]{2,1,0:T(8,128)(2,1)S(1)}) fusion(bf16[2,64,128]{2,1,0:T(8,128)(2,1)S(1)} %collective-permute-done.3, f32[3,2,64,128]{3,2,1,0:T(8,128)} %collective-permute-done.2, f32[]{:T(128)} %bitcast.54, f32[]{:T(128)} %bitcast.57, f32[]{:T(128)} %bitcast.35, ...), kind=kLoop, calls=%fused_computation.124 | loop fusion | flops 180224 | bytes 426000 | tf_op jit(solution)/shard_map/stack | solution.py:101
  118.0 18.6 %all_to_all.45 = bf16[16,2,64,128]{3,1,2,0:T(2,128)(2,1)S(1)} all-to-all(bf16[16,2,64,128]{3,1,2,0:T(2,128)(2,1)S(1)} %broadcast_in_dim.162), channel_id=1, replica_groups=mesh['xh'=2,'z'=8,'y'=8,'xl'=2,'c'=2] {'y','xl'}, dimensions={0} | all-to-all | bytes 1048576 | tf_op jit(solution)/shard_map/all_to_all | solution.py:16
  148.7 5.4 %all-gather.1 = bf16[4,64,2,128]{3,1,0,2:T(8,128)(2,1)S(1)} all-gather(bf16[2,64,2,128]{3,1,0,2:T(8,128)(2,1)S(1)} %slice.262), channel_id=3, replica_groups=mesh['xh'=2,'z'=8,'y'=8,'xl'=2,'c'=2] {'c'}, dimensions={0}, use_global_device_ids=true | all-gather | bytes 196608 | tf_op jit(solution)/shard_map/all_gather | solution.py:27
  159.1 4.2 %all-to-all-start.4 = ((bf16[16,2,64,128]{3,1,2,0:T(2,128)(2,1)}), bf16[16,2,64,128]{3,1,2,0:T(2,128)(2,1)}, u32[]{:S(2)}, u32[]{:S(2)}) async-start(bf16[16,2,64,128]{3,1,2,0:T(2,128)(2,1)} %broadcast_in_dim.163), calls=%async_computation.4 | async-start | bytes 1048576 | tf_op jit(solution)/shard_map/all_to_all | solution.py:16
  166.8 12.7 %all-to-all-done.4 = bf16[16,2,64,128]{3,1,2,0:T(2,128)(2,1)} async-done(((bf16[16,2,64,128]{3,1,2,0:T(2,128)(2,1)}), bf16[16,2,64,128]{3,1,2,0:T(2,128)(2,1)}, u32[]{:S(2)}, u32[]{:S(2)}) %all-to-all-start.4) | async-done | bytes 524320 | tf_op jit(solution)/shard_map/all_to_all | solution.py:16
  185.8 6.3 %collective-permute-done.5 = bf16[2,64,128]{2,1,0:T(8,128)(2,1)S(1)} collective-permute-done((bf16[2,64,128]{2,1,0:T(8,128)(2,1)S(1)}, bf16[2,64,128]{2,1,0:T(8,128)(2,1)S(1)}, u32[]{:S(2)}, u32[]{:S(2)}) %collective-permute-start.5) | collective-permute-done | bytes 32800 | tf_op jit(solution)/shard_map/ppermute | solution.py:117
  195.9 18.6 %all_to_all.46 = bf16[16,2,64,128]{3,1,2,0:T(2,128)(2,1)S(1)} all-to-all(bf16[16,2,64,128]{3,1,2,0:T(2,128)(2,1)S(1)} %broadcast_in_dim.164), channel_id=1, replica_groups=mesh['xh'=2,'z'=8,'y'=8,'xl'=2,'c'=2] {'y','xl'}, dimensions={0} | all-to-all | bytes 1048576 | tf_op jit(solution)/shard_map/all_to_all | solution.py:16
  228.0 5.4 %all-gather.2 = bf16[4,64,2,128]{3,1,0,2:T(8,128)(2,1)S(1)} all-gather(bf16[2,64,2,128]{3,1,0,2:T(8,128)(2,1)S(1)} %slice.274), channel_id=4, replica_groups=mesh['xh'=2,'z'=8,'y'=8,'xl'=2,'c'=2] {'c'}, dimensions={0}, use_global_device_ids=true | all-gather | bytes 196608 | tf_op jit(solution)/shard_map/all_gather | solution.py:27
  239.8 4.2 %all-to-all-start.6 = ((bf16[16,2,64,128]{3,1,2,0:T(2,128)(2,1)}), bf16[16,2,64,128]{3,1,2,0:T(2,128)(2,1)}, u32[]{:S(2)}, u32[]{:S(2)}) async-start(bf16[16,2,64,128]{3,1,2,0:T(2,128)(2,1)} %broadcast_in_dim.165), calls=%async_computation.6 | async-start | bytes 1048576 | tf_op jit(solution)/shard_map/all_to_all | solution.py:16
  246.0 14.2 %all-to-all-done.6 = bf16[16,2,64,128]{3,1,2,0:T(2,128)(2,1)} async-done(((bf16[16,2,64,128]{3,1,2,0:T(2,128)(2,1)}), bf16[16,2,64,128]{3,1,2,0:T(2,128)(2,1)}, u32[]{:S(2)}, u32[]{:S(2)}) %all-to-all-start.6) | async-done | bytes 524320 | tf_op jit(solution)/shard_map/all_to_all | solution.py:16
  266.5 6.3 %collective-permute-done.7 = bf16[2,64,128]{2,1,0:T(8,128)(2,1)S(1)} collective-permute-done((bf16[2,64,128]{2,1,0:T(8,128)(2,1)S(1)}, bf16[2,64,128]{2,1,0:T(8,128)(2,1)S(1)}, u32[]{:S(2)}, u32[]{:S(2)}) %collective-permute-start.7) | collective-permute-done | bytes 32800 | tf_op jit(solution)/shard_map/ppermute | solution.py:117
  275.4 18.2 %all_to_all.47 = bf16[16,2,64,128]{3,1,2,0:T(2,128)(2,1)S(1)} all-to-all(bf16[16,2,64,128]{3,1,2,0:T(2,128)(2,1)S(1)} %broadcast_in_dim.166), channel_id=1, replica_groups=mesh['xh'=2,'z'=8,'y'=8,'xl'=2,'c'=2] {'y','xl'}, dimensions={0} | all-to-all | bytes 1048576 | tf_op jit(solution)/shard_map/all_to_all | solution.py:16
  300.9 6.0 %all-gather.3 = bf16[4,64,2,128]{3,1,0,2:T(8,128)(2,1)S(1)} all-gather(bf16[2,64,2,128]{3,1,0,2:T(8,128)(2,1)S(1)} %slice.284), channel_id=5, replica_groups=mesh['xh'=2,'z'=8,'y'=8,'xl'=2,'c'=2] {'c'}, dimensions={0}, use_global_device_ids=true | all-gather | bytes 196608 | tf_op jit(solution)/shard_map/all_gather | solution.py:27
  312.5 16.0 %all-to-all-done.8 = bf16[16,2,64,128]{3,1,2,0:T(2,128)(2,1)S(1)} async-done(((bf16[16,2,64,128]{3,1,2,0:T(2,128)(2,1)}), bf16[16,2,64,128]{3,1,2,0:T(2,128)(2,1)S(1)}, u32[]{:S(2)}, u32[]{:S(2)}) %all-to-all-start.8) | async-done | bytes 524320 | tf_op jit(solution)/shard_map/all_to_all | solution.py:16
  330.7 4.3 %all-gather.4 = bf16[8,2,64,128]{3,2,1,0:T(8,128)(2,1)S(1)} all-gather(bf16[4,2,64,128]{3,2,1,0:T(8,128)(2,1)S(1)} %pad_maximum_fusion.3), channel_id=6, replica_groups=mesh['xh'=2,'z'=8,'y'=8,'xl'=2,'c'=2] {'c'}, dimensions={0}, use_global_device_ids=true | all-gather | bytes 393216 | tf_op jit(solution)/shard_map/all_gather | solution.py:118
  (203 shorter events, 122.2 us)
Async XLA Ops:
  2.8 29.4 %all-to-all-start = ((bf16[32,64,128]{2,1,0:T(8,128)(2,1)}), bf16[32,64,128]{2,1,0:T(8,128)(2,1)}, u32[]{:S(2)}, u32[]{:S(2)}) async-start(bf16[32,64,128]{2,1,0:T(8,128)(2,1)} %bitcast.5), calls=%async_computation | async-start | bytes 1048576 | tf_op jit(solution)/shard_map/all_to_all | solution.py:75
  16.6 5.5 %copy-start.11 = (f32[16,16]{1,0:T(8,128)S(1)}, f32[16,16]{1,0:T(8,128)}, u32[]{:S(2)}) copy-start(f32[16,16]{1,0:T(8,128)} %param.8) | copy-start | bytes 3076
  19.9 40.4 %copy-start.7 = (f32[1,4096]{1,0:T(1,128)S(1)}, f32[1,4096]{1,0:T(1,128)}, u32[]{:S(2)}) copy-start(f32[1,4096]{1,0:T(1,128)} %param.9) | copy-start | bytes 49156
  19.9 43.2 %collective-permute-start = (bf16[4096,384]{0,1:T(8,128)(2,1)S(1)}, bf16[4096,384]{0,1:T(8,128)(2,1)}, u32[]{:S(2)}, u32[]{:S(2)}) collective-permute-start(bf16[4096,384]{0,1:T(8,128)(2,1)S(1)} %bitcast.345), channel_id=1, source_target_pairs={{0,1},{1,0},{2,3},{3,2},{4,5},{5,4},{6,7},{7,6},{8,9},{9,8},{10,11... | collective-permute-start | bytes 9437192 | tf_op jit(solution)/shard_map/ppermute | solution.py:68
  35.7 22.2 %all-to-all-start.1 = ((bf16[16,2,64,128]{3,1,2,0:T(2,128)(2,1)}), bf16[16,2,64,128]{3,1,2,0:T(2,128)(2,1)}, u32[]{:S(2)}, u32[]{:S(2)}) async-start(bf16[16,2,64,128]{3,1,2,0:T(2,128)(2,1)} %broadcast_in_dim.159), calls=%async_computation.1 | async-start | bytes 1048576 | tf_op jit(solution)/shard_map/all_to_all | solution.py:16
  63.0 24.0 %slice-start = ((bf16[1,4,128,128]{3,2,1,0:T(8,128)(2,1)}), bf16[1,3,128,128]{3,2,1,0:T(8,128)(2,1)S(1)}, s32[]{:S(2)}) async-start(bf16[1,4,128,128]{3,2,1,0:T(8,128)(2,1)} %param.6), calls=%async_computation.9 | async-start | bytes 196608 | tf_op jit(solution)/shard_map/slice | solution.py:88
  80.5 20.4 %all-to-all-start.2 = ((bf16[16,2,64,128]{3,1,2,0:T(2,128)(2,1)}), bf16[16,2,64,128]{3,1,2,0:T(2,128)(2,1)}, u32[]{:S(2)}, u32[]{:S(2)}) async-start(bf16[16,2,64,128]{3,1,2,0:T(2,128)(2,1)} %broadcast_in_dim.161), calls=%async_computation.2 | async-start | bytes 1048576 | tf_op jit(solution)/shard_map/all_to_all | solution.py:16
  84.8 18.9 %collective-permute-start.1 = (bf16[4096,128]{1,0:T(8,128)(2,1)}, bf16[4096,128]{1,0:T(8,128)(2,1)}, u32[]{:S(2)}, u32[]{:S(2)}) collective-permute-start(bf16[4096,128]{1,0:T(8,128)(2,1)} %bitcast.350), channel_id=1, source_target_pairs={{0,1},{1,0},{2,3},{3,2},{4,5},{5,4},{6,7},{7,6},{8,9},{9,8},{10,11... | collective-permute-start | bytes 3145736 | tf_op jit(solution)/shard_map/ppermute | solution.py:69
  92.0 16.9 %collective-permute-start.2 = (f32[3,2,64,128]{3,2,1,0:T(8,128)}, f32[3,2,64,128]{3,2,1,0:T(8,128)}, u32[]{:S(2)}, u32[]{:S(2)}) collective-permute-start(f32[3,2,64,128]{3,2,1,0:T(8,128)} %pad_maximum_fusion.1), channel_id=1, source_target_pairs={{0,32},{32,64},{64,96},{96,128},{128,160},{160,192},{192,224},{224... | collective-permute-start | bytes 589832 | tf_op jit(solution)/shard_map/ppermute | solution.py:101
  105.3 8.3 %collective-permute-start.3 = (bf16[2,64,128]{2,1,0:T(8,128)(2,1)S(1)}, bf16[2,64,128]{2,1,0:T(8,128)(2,1)S(1)}, u32[]{:S(2)}, u32[]{:S(2)}) collective-permute-start(bf16[2,64,128]{2,1,0:T(8,128)(2,1)S(1)} %fusion.64), channel_id=1, source_target_pairs={{0,32},{32,64},{64,96},{96,128},{128,160},{160,192},{192,224},{224... | collective-permute-start | bytes 98312 | tf_op jit(solution)/shard_map/ppermute | solution.py:117
  137.2 0.8 copy-start.3
  138.0 9.3 %copy-start.12 = (pred[64,64]{0,1:T(8,128)(4,1)S(1)}, pred[64,64]{0,1:T(8,128)(4,1)}, u32[]{:S(2)}) copy-start(pred[64,64]{0,1:T(8,128)(4,1)} %iota_compare_fusion) | copy-start | bytes 12292
  159.1 20.4 %all-to-all-start.4 = ((bf16[16,2,64,128]{3,1,2,0:T(2,128)(2,1)}), bf16[16,2,64,128]{3,1,2,0:T(2,128)(2,1)}, u32[]{:S(2)}, u32[]{:S(2)}) async-start(bf16[16,2,64,128]{3,1,2,0:T(2,128)(2,1)} %broadcast_in_dim.163), calls=%async_computation.4 | async-start | bytes 1048576 | tf_op jit(solution)/shard_map/all_to_all | solution.py:16
  164.9 20.9 %collective-permute-start.4 = (f32[2,2,64,128]{3,2,1,0:T(8,128)}, f32[2,2,64,128]{3,2,1,0:T(8,128)}, u32[]{:S(2)}, u32[]{:S(2)}) collective-permute-start(f32[2,2,64,128]{3,2,1,0:T(8,128)} %pad_maximum_fusion.2), channel_id=1, source_target_pairs={{0,32},{32,64},{64,96},{96,128},{128,160},{160,192},{192,224},{224... | collective-permute-start | bytes 393224 | tf_op jit(solution)/shard_map/ppermute | solution.py:101
  183.9 8.3 %collective-permute-start.5 = (bf16[2,64,128]{2,1,0:T(8,128)(2,1)S(1)}, bf16[2,64,128]{2,1,0:T(8,128)(2,1)S(1)}, u32[]{:S(2)}, u32[]{:S(2)}) collective-permute-start(bf16[2,64,128]{2,1,0:T(8,128)(2,1)S(1)} %fusion.74), channel_id=1, source_target_pairs={{0,32},{32,64},{64,96},{96,128},{128,160},{160,192},{192,224},{224... | collective-permute-start | bytes 98312 | tf_op jit(solution)/shard_map/ppermute | solution.py:117
  215.9 10.7 %copy-start.13 = (pred[64,64]{0,1:T(8,128)(4,1)S(1)}, pred[64,64]{0,1:T(8,128)(4,1)}, u32[]{:S(2)}) copy-start(pred[64,64]{0,1:T(8,128)(4,1)} %iota_compare_fusion) | copy-start | bytes 12292
  239.8 20.4 %all-to-all-start.6 = ((bf16[16,2,64,128]{3,1,2,0:T(2,128)(2,1)}), bf16[16,2,64,128]{3,1,2,0:T(2,128)(2,1)}, u32[]{:S(2)}, u32[]{:S(2)}) async-start(bf16[16,2,64,128]{3,1,2,0:T(2,128)(2,1)} %broadcast_in_dim.165), calls=%async_computation.6 | async-start | bytes 1048576 | tf_op jit(solution)/shard_map/all_to_all | solution.py:16
  244.1 22.4 %collective-permute-start.6 = (f32[1,2,64,128]{3,2,1,0:T(8,128)}, f32[1,2,64,128]{3,2,1,0:T(8,128)}, u32[]{:S(2)}, u32[]{:S(2)}) collective-permute-start(f32[1,2,64,128]{3,2,1,0:T(8,128)} %get-tuple-element.21), channel_id=1, source_target_pairs={{0,32},{32,64},{64,96},{96,128},{128,160},{160,192},{192,224},{224... | collective-permute-start | bytes 196616 | tf_op jit(solution)/shard_map/ppermute | solution.py:101
  264.5 2.0 copy-start.5
  264.6 8.3 %collective-permute-start.7 = (bf16[2,64,128]{2,1,0:T(8,128)(2,1)S(1)}, bf16[2,64,128]{2,1,0:T(8,128)(2,1)S(1)}, u32[]{:S(2)}, u32[]{:S(2)}) collective-permute-start(bf16[2,64,128]{2,1,0:T(8,128)(2,1)S(1)} %fusion.76), channel_id=1, source_target_pairs={{0,32},{32,64},{64,96},{96,128},{128,160},{160,192},{192,224},{224... | collective-permute-start | bytes 98312 | tf_op jit(solution)/shard_map/ppermute | solution.py:117
  295.0 5.8 %copy-start.14 = (pred[64,64]{0,1:T(8,128)(4,1)S(1)}, pred[64,64]{0,1:T(8,128)(4,1)}, u32[]{:S(2)}) copy-start(pred[64,64]{0,1:T(8,128)(4,1)} %iota_compare_fusion) | copy-start | bytes 12292
  297.5 15.0 %copy-start.6 = (f32[1,64,128]{2,1,0:T(8,128)S(1)}, f32[1,64,128]{2,1,0:T(8,128)}, u32[]{:S(2)}) copy-start(f32[1,64,128]{2,1,0:T(8,128)} %copy-done.5) | copy-start | bytes 98308
  300.7 28.0 %copy-start = (bf16[1,4096,128]{2,1,0:T(8,128)(2,1)S(1)}, bf16[1,4096,128]{2,1,0:T(8,128)(2,1)}, u32[]{:S(2)}) copy-start(bf16[1,4096,128]{2,1,0:T(8,128)(2,1)} %param.11) | copy-start | bytes 3145732
  308.9 19.7 %all-to-all-start.8 = ((bf16[16,2,64,128]{3,1,2,0:T(2,128)(2,1)}), bf16[16,2,64,128]{3,1,2,0:T(2,128)(2,1)S(1)}, u32[]{:S(2)}, u32[]{:S(2)}) async-start(bf16[16,2,64,128]{3,1,2,0:T(2,128)(2,1)} %broadcast_in_dim.167), calls=%async_computation.8 | async-start | bytes 1048576 | tf_op jit(solution)/shard_map/all_to_all | solution.py:16
  (6 other events, 4.3 us)
